TPU v7x, 32 devices: a 4x2x2 block of a 4x4x8 slice. The times are simulated.
32 devices in a mesh: dp: 4 (over y, z), fsdp: 8 (over x, core).
Axes of the slice: x: 4, y: 2, z: 2, core: 2. Of those that a mesh axis runs over, the one named last changes fastest.
The devices are a block of a 4x4x8 slice.
Arguments:
- prompts: bfloat16 [128, 512, 2048], P(('dp', 'fsdp')), parts along dimension 0
- ln1_gain: bfloat16 [2048], P('fsdp')
- ln1_bias: bfloat16 [2048], P('fsdp')
- w_qkv: bfloat16 [2048, 3, 32, 64], P('fsdp')
- b_qkv: bfloat16 [6144], P('fsdp')
- w_out: bfloat16 [2048, 2048], P('fsdp')
- b_out: bfloat16 [2048], P('fsdp')
- ln2_gain: bfloat16 [2048], P('fsdp')
- ln2_bias: bfloat16 [2048], P('fsdp')
- w_up: bfloat16 [2048, 8192], P('fsdp')
- b_up: bfloat16 [8192], P('fsdp')
- w_down: bfloat16 [8192, 2048], P('fsdp')
- b_down: bfloat16 [2048], P('fsdp')
Outputs:
- output 1: bfloat16 [128, 512, 2048], P(('dp', 'fsdp')), parts along dimension 0
- output 2: bfloat16 [128, 512, 32, 64], P(('dp', 'fsdp')), parts along dimension 0
- output 3: bfloat16 [128, 512, 32, 64], P(('dp', 'fsdp')), parts along dimension 0
There are 4 independent parts. A program takes and returns all parts, laid end to end along the dimension named above; an argument that names none is the same for every part.
All inputs are finite; a program needn't handle non-finite values.
Results may differ from a plain program's by a relative error of at most 0.00848424.
Values are sent between devices in bfloat16 or wider.
A program may use at most 768 MiB of HBM per device.

v0:
```python
import jax
import jax.numpy as jnp
from jax import lax
from jax.sharding import PartitionSpec as P

LN_EPS = 1e-5
QUERY_BLOCK = 256


def layer_norm(act, gain, shift):
    act_f32 = act.astype(jnp.float32)
    mean_val = jnp.mean(act_f32, axis=-1, keepdims=True)
    centered = act_f32 - mean_val
    var_val = jnp.mean(centered * centered, axis=-1, keepdims=True)
    normed = centered * lax.rsqrt(var_val + LN_EPS)
    return (normed * gain.astype(jnp.float32) + shift.astype(jnp.float32)).astype(jnp.bfloat16)


def causal_attention(queries, keys, values):
    seq_len = queries.shape[1]
    q_block = min(seq_len, QUERY_BLOCK)
    scale = queries.shape[-1] ** -0.5
    key_pos = jnp.arange(seq_len)

    def one_block(blk_idx):
        start = blk_idx * q_block
        q_blk = lax.dynamic_slice_in_dim(queries, start, q_block, axis=1)
        scores = jnp.einsum('bqhe,bkhe->bhqk', q_blk, keys, preferred_element_type=jnp.float32) * scale
        allowed = key_pos[None, :] <= (start + jnp.arange(q_block))[:, None]
        scores = jnp.where(allowed, scores, -jnp.inf)
        probs = jax.nn.softmax(scores, axis=-1).astype(jnp.bfloat16)
        return jnp.einsum('bhqk,bkhe->bqhe', probs, values, preferred_element_type=jnp.float32).astype(jnp.bfloat16)

    return lax.map(one_block, jnp.arange(seq_len // q_block))


def solution(mesh):
    batch_axes = ('dp', 'fsdp')

    def gather_full(shard):
        return lax.all_gather(shard, 'fsdp', axis=0, tiled=True)

    def local_layer(prompts, ln1_gain, ln1_bias, w_qkv, b_qkv, w_out, b_out, ln2_gain, ln2_bias, w_up, b_up, w_down, b_down):
        batch_loc, seq_len, d_model = prompts.shape
        heads, head_dim = w_qkv.shape[2], w_qkv.shape[3]
        normed1 = layer_norm(prompts, gather_full(ln1_gain), gather_full(ln1_bias))
        w_qkv_full = gather_full(w_qkv)
        b_qkv_full = gather_full(b_qkv)
        proj_qkv = jnp.einsum('bsd,djhe->jbshe', normed1, w_qkv_full, preferred_element_type=jnp.float32)
        proj_qkv = (proj_qkv + b_qkv_full.astype(jnp.float32).reshape(3, 1, 1, heads, head_dim)).astype(jnp.bfloat16)
        ctx_blocks = causal_attention(proj_qkv[0], proj_qkv[1], proj_qkv[2])
        w_out_full = gather_full(w_out).reshape(heads, head_dim, d_model)
        b_out_full = gather_full(b_out)
        attn_out = jnp.einsum('nbqhe,hec->bnqc', ctx_blocks, w_out_full, preferred_element_type=jnp.float32).reshape(batch_loc, seq_len, d_model)
        resid = (prompts.astype(jnp.float32) + attn_out + b_out_full.astype(jnp.float32)).astype(jnp.bfloat16)
        normed2 = layer_norm(resid, gather_full(ln2_gain), gather_full(ln2_bias))
        w_up_full = gather_full(w_up)
        b_up_full = gather_full(b_up)
        hidden = jnp.einsum('bsd,df->bsf', normed2, w_up_full, preferred_element_type=jnp.float32) + b_up_full.astype(jnp.float32)
        hidden = jax.nn.gelu(hidden, approximate=True).astype(jnp.bfloat16)
        w_down_full = gather_full(w_down)
        b_down_full = gather_full(b_down)
        mlp_out = jnp.einsum('bsf,fd->bsd', hidden, w_down_full, preferred_element_type=jnp.float32)
        layer_out = (resid.astype(jnp.float32) + mlp_out + b_down_full.astype(jnp.float32)).astype(jnp.bfloat16)
        return layer_out, proj_qkv[1], proj_qkv[2]

    weight_spec = P('fsdp')
    return jax.shard_map(local_layer, mesh=mesh, in_specs=(P(batch_axes),) + (weight_spec,) * 12, out_specs=(P(batch_axes), P(batch_axes), P(batch_axes)), check_vma=False)
```

profile of v0, /device:TPU:81, one launch (start us, length us, event | category | flops | bytes accessed | tf_op | source)
XLA Modules:
  0.0 586.2 jit_solution(6696221271504844270)
XLA Ops:
  10.3 4.5 convert_reduce_fusion.1
  14.9 5.7 fusion.55
  20.6 14.9 %all-gather.2 = bf16[8,1,768]{2,1,0:T(2,128)(2,1)S(1)} all-gather(bf16[1,1,768]{2,1,0:T(2,128)(2,1)S(1)} %reshape.61), channel_id=1, replica_groups=mesh['dp'=4,'fsdp'=8] {'fsdp'}, dimensions={0}, use_global_device_ids=true | all-gather | bytes 13824 | tf_op jit(solution)/shard_map/all_gather | solution.py:41
  35.6 10.5 %all-gather = bf16[8,1,256]{2,1,0:T(2,128)(2,1)S(1)} all-gather(bf16[1,1,256]{2,1,0:T(2,128)(2,1)S(1)} %reshape.57), channel_id=1, replica_groups=mesh['dp'=4,'fsdp'=8] {'fsdp'}, dimensions={0}, use_global_device_ids=true | all-gather | bytes 4608 | tf_op jit(solution)/shard_map/all_gather | solution.py:41
  46.1 8.3 %all-gather.1 = bf16[8,1,256]{2,1,0:T(2,128)(2,1)S(1)} all-gather(bf16[1,1,256]{2,1,0:T(2,128)(2,1)S(1)} %reshape.59), channel_id=1, replica_groups=mesh['dp'=4,'fsdp'=8] {'fsdp'}, dimensions={0}, use_global_device_ids=true | all-gather | bytes 4608 | tf_op jit(solution)/shard_map/all_gather | solution.py:41
  54.5 9.6 %all-gather.3 = bf16[8,1,256]{2,1,0:T(2,128)(2,1)S(1)} all-gather(bf16[1,1,256]{2,1,0:T(2,128)(2,1)S(1)} %reshape.63), channel_id=1, replica_groups=mesh['dp'=4,'fsdp'=8] {'fsdp'}, dimensions={0}, use_global_device_ids=true | all-gather | bytes 4608 | tf_op jit(solution)/shard_map/all_gather | solution.py:41
  64.6 12.9 %all_gather.45 = bf16[8192]{0:T(1024)(128)(2,1)S(1)} all-gather(bf16[1024]{0:T(1024)(128)(2,1)S(1)} %copy-done.7), channel_id=1, replica_groups=mesh['dp'=4,'fsdp'=8] {'fsdp'}, dimensions={0}, use_global_device_ids=true | all-gather | bytes 18432 | tf_op jit(solution)/shard_map/all_gather | solution.py:41
  78.2 8.3 %all-gather.4 = bf16[8,1,256]{2,1,0:T(2,128)(2,1)S(1)} all-gather(bf16[1,1,256]{2,1,0:T(2,128)(2,1)S(1)} %reshape.65), channel_id=1, replica_groups=mesh['dp'=4,'fsdp'=8] {'fsdp'}, dimensions={0}, use_global_device_ids=true | all-gather | bytes 4608 | tf_op jit(solution)/shard_map/all_gather | solution.py:41
  87.1 9.6 %all-gather.5 = bf16[8,1,256]{2,1,0:T(2,128)(2,1)S(1)} all-gather(bf16[1,1,256]{2,1,0:T(2,128)(2,1)S(1)} %reshape.67), channel_id=1, replica_groups=mesh['dp'=4,'fsdp'=8] {'fsdp'}, dimensions={0}, use_global_device_ids=true | all-gather | bytes 4608 | tf_op jit(solution)/shard_map/all_gather | solution.py:41
  97.3 8.4 %all-gather.6 = bf16[8,1,256]{2,1,0:T(2,128)(2,1)S(1)} all-gather(bf16[1,1,256]{2,1,0:T(2,128)(2,1)S(1)} %reshape.69), channel_id=1, replica_groups=mesh['dp'=4,'fsdp'=8] {'fsdp'}, dimensions={0}, use_global_device_ids=true | all-gather | bytes 4608 | tf_op jit(solution)/shard_map/all_gather | solution.py:41
  106.3 32.4 %all-gather.12.cloned.1.call-done = bf16[2048,3,32,64]{0,3,2,1:T(8,128)(2,1)} async-done(((bf16[256,3,32,64]{0,3,2,1:T(8,128)(2,1)}), bf16[2048,3,32,64]{0,3,2,1:T(8,128)(2,1)}) %all-gather.12.cloned.1.call-update) | async-done | bytes 25165840 | tf_op jit(solution)/shard_map/all_gather | solution.py:41
  138.7 61.9 %fusion.44 = bf16[3,4,512,32,64]{2,4,3,0,1:T(8,128)(2,1)} fusion(f32[3,32,64]{2,1,0:T(8,128)S(1)} %reshape.56, bf16[2048,3,32,64]{0,3,2,1:T(8,128)(2,1)} %all-gather.12.cloned.1.call-done, bf16[4,512,2048]{2,1,0:T(8,128)(2,1)} %param.15, f32[2048]{0:T(1024)S(1)} %bitcast.83, f32[2048]{0:T(1024)S(1)} %bitcast.82, f32[4,512]{1,0:T(4,128)S(1)} %add_rsqrt_fusion.1, ...), kind=kOutput, calls=%fused_computation.39 | convolution fusion | flops 51589939200 | bytes 58777600 | tf_op jit(solution)/shard_map/bsd,djhe->jbshe/dot_general | solution.py:49
  200.6 16.7 %slice_bitcast_fusion = (bf16[4,512,32,64]{1,3,2,0:T(8,128)(2,1)}, bf16[4,512,32,64]{1,3,2,0:T(8,128)(2,1)}, bf16[4,512,32,64]{1,3,2,0:T(8,128)(2,1)}) fusion(bf16[3,4,512,32,64]{2,4,3,0,1:T(8,128)(2,1)} %fusion.44), kind=kLoop, calls=%fused_computation.65 | loop fusion | bytes 50331648 | tf_op jit(solution)/shard_map/squeeze | solution.py:51
  217.3 124.9 %while.11 = (s32[]{:T(128)}, bf16[2,4,256,32,64]{2,4,3,1,0:T(8,128)(2,1)}, s32[2]{0:T(128)S(1)}, bf16[4,512,32,64]{1,3,2,0:T(8,128)(2,1)}, bf16[4,512,32,64]{1,3...) while((s32[]{:T(128)}, ...), condition=%wide.region_5.6_spmd.clone, body=%wide.region_2.5_spmd.clone.sunk | while | flops 4397859840 | bytes 159910560 | solution.py:34
  219.0 33.9 %fusion.125 = (f32[4,32,256]{2,1,0:T(8,128)S(1)}, f32[4,32,256,512]{3,2,1,0:T(8,128)}) fusion(pred[256,512]{1,0:T(8,128)(4,1)S(1)} %iota_compare_fusion.2, bf16[4,512,32,64]{1,3,2,0:T(8,128)(2,1)} %get-tuple-element.139, bf16[4,512,32,64]{1,3,2,0:T(8,128)(2,1)} %get-tuple-element.138, s32[]{:T(128)S(6)} %select_n.22), kind=kOutput, calls=%fused_computation.86.clone.1 | convolution fusion | flops 2214593024 | bytes 79953920 | tf_op jit(solution)/shard_map/while/body/eval_jaxpr/sub | solution.py:31
  252.9 27.0 %bitcast_dynamic-update-slice_fusion.2 = bf16[2,4,256,32,64]{2,4,3,1,0:T(8,128)(2,1)} fusion(bf16[2,4,256,32,64]{2,4,3,1,0:T(8,128)(2,1)} %get-tuple-element.126, s32[]{:T(128)} %get-tuple-element.125, bf16[4,512,32,64]{1,3,2,0:T(8,128)(2,1)} %get-tuple-element.140, f32[4,32,256,512]{3,2,1,0:T(8,128)} %get-tuple-element.113, ...), kind=kOutput, calls=%fused_computation.11.clone.1 | convolution fusion | flops 2183135232 | bytes 79823360 | tf_op jit(solution)/shard_map/while/body/eval_jaxpr/bhqk,bkhe->bqhe/dot_general | solution.py:32
  281.3 33.9 %fusion.125 = (f32[4,32,256]{2,1,0:T(8,128)S(1)}, f32[4,32,256,512]{3,2,1,0:T(8,128)}) fusion(pred[256,512]{1,0:T(8,128)(4,1)S(1)} %iota_compare_fusion.2, bf16[4,512,32,64]{1,3,2,0:T(8,128)(2,1)} %get-tuple-element.139, bf16[4,512,32,64]{1,3,2,0:T(8,128)(2,1)} %get-tuple-element.138, s32[]{:T(128)S(6)} %select_n.22), kind=kOutput, calls=%fused_computation.86.clone.1 | convolution fusion | flops 2214593024 | bytes 79953920 | tf_op jit(solution)/shard_map/while/body/eval_jaxpr/sub | solution.py:31
  315.2 27.0 %bitcast_dynamic-update-slice_fusion.2 = bf16[2,4,256,32,64]{2,4,3,1,0:T(8,128)(2,1)} fusion(bf16[2,4,256,32,64]{2,4,3,1,0:T(8,128)(2,1)} %get-tuple-element.126, s32[]{:T(128)} %get-tuple-element.125, bf16[4,512,32,64]{1,3,2,0:T(8,128)(2,1)} %get-tuple-element.140, f32[4,32,256,512]{3,2,1,0:T(8,128)} %get-tuple-element.113, ...), kind=kOutput, calls=%fused_computation.11.clone.1 | convolution fusion | flops 2183135232 | bytes 79823360 | tf_op jit(solution)/shard_map/while/body/eval_jaxpr/bhqk,bkhe->bqhe/dot_general | solution.py:32
  342.2 24.3 %convolution_bitcast_fusion = f32[4,2,256,2048]{3,2,0,1:T(8,128)} fusion(bf16[2,4,256,32,64]{2,4,3,1,0:T(8,128)(2,1)} %get-tuple-element.40, bf16[32,64,2048,1,1]{2,1,0,4,3:T(8,128)(2,1)} %bitcast.84), kind=kOutput, calls=%fused_computation.76 | convolution fusion | flops 17179869184 | bytes 33554432 | tf_op jit(solution)/shard_map/nbqhe,hec->bnqc/dot_general | solution.py:54
  366.5 7.6 %copy.17 = f32[4,2,256,2048]{3,2,1,0:T(8,128)S(1)} copy(f32[4,2,256,2048]{3,2,0,1:T(8,128)} %convolution_bitcast_fusion) | data formatting | bytes 33554432 | tf_op jit(solution)/shard_map/nbqhe,hec->bnqc/transpose | solution.py:54
  374.8 4.5 convert_reduce_fusion
  385.1 98.2 %fusion.116 = bf16[4,512,8192]{2,1,0:T(8,128)(2,1)} fusion(bf16[2048,8192]{1,0:T(8,128)(2,1)} %all-gather.16.cloned.1.call-done, f32[8192]{0:T(1024)S(1)} %copy-done.2, bf16[4,512,2048]{2,1,0:T(8,128)(2,1)} %copy-done.1, f32[2048]{0:T(1024)S(1)} %bitcast.81, f32[2048]{0:T(1024)S(1)} %bitcast.79, f32[4,512]{1,0:T(4,128)S(1)} %add_rsqrt_fusion, ...), kind=kOutput, calls=%fused_computation.29.clone.clone.clone.clone.1 | convolution fusion | flops 68912414720 | bytes 75563008 | tf_op jit(solution)/shard_map/bsd,df->bsf/dot_general | solution.py:59
  483.3 16.0 %all-gather.18.cloned.1.call-done = bf16[8192,2048]{1,0:T(8,128)(2,1)} async-done(((bf16[1024,2048]{1,0:T(8,128)(2,1)}), bf16[8192,2048]{1,0:T(8,128)(2,1)}) %all-gather.18.cloned.1.call-update) | async-done | bytes 33554448 | tf_op jit(solution)/shard_map/all_gather | solution.py:41
  499.2 80.2 %fusion.62 = bf16[4,512,2048]{2,1,0:T(8,128)(2,1)} fusion(bf16[4,512,2048]{2,1,0:T(8,128)(2,1)} %copy-done.1, f32[2048]{0:T(1024)S(1)} %bitcast.80, bf16[8192,2048]{1,0:T(8,128)(2,1)} %all-gather.18.cloned.1.call-done, bf16[4,512,8192]{2,1,0:T(8,128)(2,1)} %fusion.116), kind=kOutput, calls=%fused_computation.63 | convolution fusion | flops 68736253952 | bytes 83894272 | tf_op jit(solution)/shard_map/bsf,fd->bsd/dot_general | solution.py:63
  (69 shorter events, 14.1 us)
Async XLA Ops:
  7.2 13.4 %copy-start.8 = (bf16[768]{0:T(1024)(128)(2,1)S(1)}, bf16[768]{0:T(1024)(128)(2,1)}, u32[]{:S(2)}) copy-start(bf16[768]{0:T(1024)(128)(2,1)} %param.19) | copy-start | bytes 4612
  7.2 28.4 %copy-start.9 = (bf16[256]{0:T(256)(128)(2,1)S(1)}, bf16[256]{0:T(256)(128)(2,1)}, u32[]{:S(2)}) copy-start(bf16[256]{0:T(256)(128)(2,1)} %param.16) | copy-start | bytes 1540
  7.2 38.9 %copy-start.10 = (bf16[256]{0:T(256)(128)(2,1)S(1)}, bf16[256]{0:T(256)(128)(2,1)}, u32[]{:S(2)}) copy-start(bf16[256]{0:T(256)(128)(2,1)} %param.17) | copy-start | bytes 1540
  7.2 47.2 %copy-start.11 = (bf16[256]{0:T(256)(128)(2,1)S(1)}, bf16[256]{0:T(256)(128)(2,1)}, u32[]{:S(2)}) copy-start(bf16[256]{0:T(256)(128)(2,1)} %param.21) | copy-start | bytes 1540
  7.2 57.4 %copy-start.7 = (bf16[1024]{0:T(1024)(128)(2,1)S(1)}, bf16[1024]{0:T(1024)(128)(2,1)}, u32[]{:S(2)}) copy-start(bf16[1024]{0:T(1024)(128)(2,1)} %param.25) | copy-start | bytes 6148
  7.2 71.0 %copy-start.12 = (bf16[256]{0:T(256)(128)(2,1)S(1)}, bf16[256]{0:T(256)(128)(2,1)}, u32[]{:S(2)}) copy-start(bf16[256]{0:T(256)(128)(2,1)} %param.22) | copy-start | bytes 1540
  7.2 79.9 %copy-start.13 = (bf16[256]{0:T(256)(128)(2,1)S(1)}, bf16[256]{0:T(256)(128)(2,1)}, u32[]{:S(2)}) copy-start(bf16[256]{0:T(256)(128)(2,1)} %param.23) | copy-start | bytes 1540
  7.3 90.0 %copy-start.14 = (bf16[256]{0:T(256)(128)(2,1)S(1)}, bf16[256]{0:T(256)(128)(2,1)}, u32[]{:S(2)}) copy-start(bf16[256]{0:T(256)(128)(2,1)} %param.27) | copy-start | bytes 1540
  7.3 131.4 %all-gather.12.cloned.1.call-start = ((), (), s32[]{:S(2)}) async-start(), calls=%async_computation | async-start | bytes 28311552 | tf_op jit(solution)/shard_map/all_gather | solution.py:41
  8.1 334.2 %all-gather.14.cloned.1.call-start = ((), (), s32[]{:S(2)}) async-start(), calls=%async_computation.1 | async-start | bytes 9437184 | tf_op jit(solution)/shard_map/all_gather | solution.py:41
  8.9 376.2 %all-gather.16.cloned.1.call-start = ((), (), s32[]{:S(2)}) async-start(), calls=%async_computation.2 | async-start | bytes 37748736 | tf_op jit(solution)/shard_map/all_gather | solution.py:41
  9.7 489.6 %all-gather.18.cloned.1.call-start = ((), (), s32[]{:S(2)}) async-start(), calls=%async_computation.3 | async-start | bytes 37748736 | tf_op jit(solution)/shard_map/all_gather | solution.py:41
  366.5 8.2 %copy-start = (bf16[4,512,2048]{2,1,0:T(8,128)(2,1)S(1)}, bf16[4,512,2048]{2,1,0:T(8,128)(2,1)}, u32[]{:S(2)}) copy-start(bf16[4,512,2048]{2,1,0:T(8,128)(2,1)} %param.15) | copy-start | bytes 25165828
  366.5 8.2 %copy-start.3 = (f32[8,1,256]{2,1,0:T(1,128)S(1)}, f32[8,1,256]{2,1,0:T(1,128)}, u32[]{:S(2)}) copy-start(f32[8,1,256]{2,1,0:T(1,128)} %convert_element_type.78) | copy-start | bytes 24580
  374.7 10.3 %copy-start.2 = (f32[8192]{0:T(1024)S(1)}, f32[8192]{0:T(1024)}, u32[]{:S(2)}) copy-start(f32[8192]{0:T(1024)} %convert_element_type.72) | copy-start | bytes 98308
  374.7 10.3 %copy-start.4 = (f32[8,1,256]{2,1,0:T(1,128)S(1)}, f32[8,1,256]{2,1,0:T(1,128)}, u32[]{:S(2)}) copy-start(f32[8,1,256]{2,1,0:T(1,128)} %convert_element_type.79) | copy-start | bytes 24580
  374.7 10.3 %copy-start.6 = (f32[8,1,256]{2,1,0:T(1,128)S(1)}, f32[8,1,256]{2,1,0:T(1,128)}, u32[]{:S(2)}) copy-start(f32[8,1,256]{2,1,0:T(1,128)} %convert_element_type.80) | copy-start | bytes 24580
  379.3 3.4 copy-start.1
  385.1 114.1 %copy-start.5 = (f32[8,1,256]{2,1,0:T(1,128)S(1)}, f32[8,1,256]{2,1,0:T(1,128)}, u32[]{:S(2)}) copy-start(f32[8,1,256]{2,1,0:T(1,128)} %convert_element_type.81) | copy-start | bytes 24580
Sparse Core Ops, SparseCore 0:
  9.7 128.9 all-gather.11
  140.3 47.2 all-gather.13
  189.2 153.8 all-gather.15
  344.6 154.5 all-gather.17
where the time goes:
time: 593 us; the launch traced here: 586 us
  matrix products  386 us (65%)
  blocking collectives  82.4 us (14%)
  waiting for transfers between devices  51.1 us (9%)
  local copies, waits for them, and re-layouts  29.7 us (5%)
  other arithmetic  20.5 us (3%)
  between operations  14.2 us (2%)
    dot_general x1, matrix products, local_layer(): jnp.einsum('bsd,df->bsf', normed2, w_up_full, preferred_element_type=jnp....  98.2 us
    all_gather x8, blocking collectives, gather_full(): return lax.all_gather(shard, 'fsdp', axis=0, tiled=True)  82.4 us
    dot_general x1, matrix products, local_layer(): jnp.einsum('bsf,fd->bsd', hidden, w_down_full, preferred_element_type=jnp...  80.2 us
    sub x2, matrix products, one_block(): probs = jax.nn.softmax(scores, axis=-1).astype(jnp.bfloat16)  67.8 us
    dot_general x1, matrix products, local_layer(): jnp.einsum('bsd,djhe->jbshe', normed1, w_qkv_full, preferred_element_type...  61.9 us
    dot_general x2, matrix products, one_block(): jnp.einsum('bhqk,bkhe->bqhe', probs, values, preferred_element_type=jnp.f...  54 us
    all_gather x4, waiting for transfers between devices, gather_full(): return lax.all_gather(shard, 'fsdp', axis=0, tiled=True)  48.3 us
    dot_general x1, matrix products, local_layer(): jnp.einsum('nbqhe,hec->bnqc', ctx_blocks, w_out_full, preferred_element_t...  24.3 us
  transfers between devices with their start and end apart: 4, of which 2 were waited for; matrix products, arithmetic and copies ran while one was open for 60% of the time, Pallas kernels for 0%

commit v1 on v0

v1 whole, which is shorter than its diff:
```python
import functools

import jax
import jax.numpy as jnp
from jax import lax
from jax.experimental import pallas as pl
from jax.experimental.pallas import tpu as pltpu
from jax.sharding import PartitionSpec as P

LN_EPS = 1e-5
LOG2E = 1.4426950408889634
MESH = pl.DeviceIdType.MESH
ANY = pl.BlockSpec(memory_space=pl.ANY)
SLOTS = 14
VMEM_LIMIT = 64 * 1024 * 1024 - 128 * 1024


def _nt(a, b):
    return lax.dot_general(a, b, (((1,), (1,)), ((), ())), preferred_element_type=jnp.float32)


class Where:
    def __init__(self, n):
        self.n = n
        self.g = lax.axis_index('dp')
        self.f = lax.axis_index('fsdp')
        self.p = lax.rem(self.g, 2)
        self.left = lax.rem(self.f + n - 2, n)
        self.right = lax.rem(self.f + 2, n)
        self.opp = lax.rem(self.f + n // 2, n)
        self.peer = self.f + 1 - 2 * lax.rem(self.f, 2)
        self.gz = self.g + 1 - 2 * self.p

    def greet(self, everyone):
        bar = pltpu.get_barrier_semaphore()
        if everyone:
            ids = [(self.g, lax.rem(self.f + r, self.n)) for r in range(1, self.n)]
        else:
            ids = [(self.g, self.left), (self.g, self.right), (self.g, self.peer)]
        ids.append((self.gz, self.f))
        for d in ids:
            pl.semaphore_signal(bar, inc=1, device_id=d, device_id_type=MESH)
        pl.semaphore_wait(bar, len(ids))


class Gather:
    def __init__(self, w, total, src, dst, send, recv):
        self.w, self.total, self.src, self.dst, self.send, self.recv = w, total, src, dst, send, recv

    def copy(self, c, k):
        w, p = self.w, self.w.p
        right, left, peer, pair = (w.g, w.right), (w.g, w.left), (w.g, w.peer), (w.gz, w.f)
        if k <= 2:
            to = (right, left, peer)[k]
            q, n = (p, 3) if k < 2 else (0, 4)
            a, b = self.src(c, q, n), self.dst(c, w.f, q, n)
        else:
            dev, q, n, to = {
                3: (w.left, 2 * p, 1, right),
                4: (w.right, 2 * p + 1, 1, left),
                5: (w.left, 3 * p, 1, pair),
                6: (w.right, 3 * p, 1, pair),
                7: (w.opp, 2 * p, 2, pair),
                8: (w.left, p, 3, peer),
                9: (w.right, p, 3, peer),
                10: (w.opp, 2 * p, 2, peer),
                11: (w.left, 3 - 3 * p, 1, peer),
                12: (w.right, 3 - 3 * p, 1, peer),
                13: (w.opp, 2 - 2 * p, 2, peer),
            }[k]
            a = b = self.dst(c, dev, q, n)
        return pltpu.make_async_remote_copy(
            src_ref=a, dst_ref=b, send_sem=self.send.at[c, k], recv_sem=self.recv.at[c, k], device_id=to, device_id_type=MESH)

    def start(self, c, ks):
        for k in ks:
            self.copy(c, k).start()

    def arrive(self, c, ks):
        for k in ks:
            self.copy(c, k).wait_recv()

    def prelude(self):
        for c in range(min(2, self.total)):
            self.start(c, (0, 1, 2))

    def _when(self, c, fn):
        if isinstance(c, int):
            if 0 <= c < self.total:
                fn(c)
        else:
            pl.when(jnp.logical_and(c >= 0, c < self.total))(lambda: fn(c))

    def tick(self, t):
        def done(c):
            self.arrive(c, (2, 8, 9, 10, 11, 12, 13))
            for k in range(SLOTS):
                self.copy(c, k).wait_send()

        def far(c):
            self.arrive(c, (5, 6, 7))
            self.start(c, (11, 12, 13))

        def mid(c):
            self.arrive(c, (3, 4))
            self.start(c, (7, 10))

        def near(c):
            self.arrive(c, (0, 1))
            self.start(c, (3, 4, 5, 6, 8, 9))

        self._when(t - 3, done)
        self._when(t - 2, far)
        self._when(t - 1, mid)
        self._when(t, near)
        nxt = t + 2
        if isinstance(t, int):
            if nxt < self.total:
                self.start(nxt, (0, 1, 2))
        else:
            pl.when(nxt < self.total)(lambda: self.start(nxt, (0, 1, 2)))

    @property
    def ticks(self):
        return self.total + 3


def _sems(n):
    return [pltpu.SemaphoreType.DMA((n, SLOTS)), pltpu.SemaphoreType.DMA((n, SLOTS))]


def _row_src(refs_cols):
    def src(c, q, n):
        ref, c0, width = refs_cols[c]
        u = width // 4
        return ref.at[:, pl.ds(pl.multiple_of(c0 + q * u, 128), n * u)]

    return src


def _row_dst(bufs, depth):
    def dst(c, dev, q, n):
        u = bufs[c].shape[1] // 4
        return bufs[c].at[pl.ds(pl.multiple_of(dev * depth, depth), depth), pl.ds(pl.multiple_of(q * u, 128), n * u)]

    return dst


def _ln(xf, gain, shift):
    mean = jnp.mean(xf, axis=-1, keepdims=True)
    cen = xf - mean
    var = jnp.mean(cen * cen, axis=-1, keepdims=True)
    return (cen * lax.rsqrt(var + LN_EPS) * gain + shift).astype(jnp.bfloat16)


def qkv_kernel(cfg, x_ref, w_ref, small_ref, qt, kt, vt, small_out, wbuf, hbuf, xbuf, sbuf, bias, obuf, xsem, ssend, srecv, lsem, osem, send, recv):
    n, rows, batch, seq, nchunks, brow = cfg
    w = Where(n)
    d_model = hbuf.shape[1]
    depth = d_model // n
    w.greet(True)

    def src(c, q, m):
        return w_ref.at[pl.ds(pl.multiple_of(c * rows + q * (rows // 4), 16), m * (rows // 4)), :]

    def dst(c, dev, q, m):
        return wbuf.at[pl.ds(pl.multiple_of(c * rows + q * (rows // 4), 16), m * (rows // 4)), pl.ds(pl.multiple_of(dev * depth, 128), depth)]

    ga = Gather(w, nchunks, src, dst, send, recv)

    def lanes(dev):
        return sbuf.at[:, pl.ds(pl.multiple_of(dev * depth, 128), depth)]

    smalls = []
    for r in range(1, n):
        cp = pltpu.make_async_remote_copy(
            src_ref=small_ref, dst_ref=lanes(w.f), send_sem=ssend.at[r], recv_sem=srecv.at[r],
            device_id=(w.g, lax.rem(w.f + r, n)), device_id_type=MESH)
        cp.start()
        smalls.append(cp)
    ga.prelude()
    own_small = pltpu.make_async_copy(small_ref, lanes(w.f), lsem.at[0])
    own_small.start()
    own_w = pltpu.make_async_copy(w_ref, wbuf.at[:, pl.ds(pl.multiple_of(w.f * depth, 128), depth)], lsem.at[1])
    own_w.start()

    blk = xbuf.shape[1]
    nblk = hbuf.shape[0] // blk

    def xcopy(i, slot):
        return pltpu.make_async_copy(x_ref.at[pl.ds(pl.multiple_of(i * blk, blk), blk), :], xbuf.at[slot], xsem.at[slot])

    xcopy(0, 0).start()
    own_small.wait()
    for cp in smalls:
        cp.wait()
    put_small = pltpu.make_async_copy(sbuf, small_out, lsem.at[2])
    put_small.start()
    gain = sbuf[pl.ds(0, 1), :].astype(jnp.float32)
    shift = sbuf[pl.ds(1, 1), :].astype(jnp.float32)

    def ln_step(i, _):
        slot = lax.rem(i, 2)

        @pl.when(i + 1 < nblk)
        def _():
            xcopy(i + 1, 1 - slot).start()

        xcopy(i, slot).wait()
        hbuf[pl.ds(pl.multiple_of(i * blk, blk), blk), :] = _ln(xbuf[slot].astype(jnp.float32), gain, shift)
        return 0

    lax.fori_loop(0, nblk, ln_step, 0)
    own_w.wait()

    total_rows = nchunks * rows
    per = total_rows // n // depth
    for m in range(n * per):
        j, r = m // per, m % per
        row = sbuf[pl.ds(brow + r, 1), pl.ds(j * depth, depth)].astype(jnp.float32)
        bias[pl.ds(m * depth, depth), :] = jnp.broadcast_to(row, (128, depth)).T

    def ocopy(ref, c_in, b, slot):
        return pltpu.make_async_copy(obuf.at[slot], ref.at[b, pl.ds(pl.multiple_of(c_in * rows, rows), rows), :], osem.at[slot])

    per_out = nchunks // 3

    def chunk_step(i, _):
        ga.tick(i)
        c = i - 3

        @pl.when(c >= 0)
        def _():
            def one(b, _):
                slot = lax.rem(b, 2)

                @pl.when(jnp.logical_or(c > 0, b >= 2))
                def _():
                    ocopy(qt, 0, 0, slot).wait()

                sub = 256
                for s in range(rows // sub):
                    r0 = pl.multiple_of(c * rows + s * sub, sub)
                    acc = _nt(wbuf[pl.ds(r0, sub), :], hbuf[pl.ds(pl.multiple_of(b * seq, seq), seq), :])
                    bcol = bias[pl.ds(r0, sub), :]
                    acc = acc + jnp.concatenate([bcol] * (seq // 128), axis=1)
                    obuf[slot, pl.ds(s * sub, sub), :] = acc.astype(jnp.bfloat16)
                c_in = lax.rem(c, per_out)
                for o, ref in enumerate((qt, kt, vt)):
                    @pl.when(lax.div(c, per_out) == o)
                    def _():
                        ocopy(ref, c_in, b, slot).start()
                return 0

            lax.fori_loop(0, batch, one, 0)

        return 0

    lax.fori_loop(0, ga.ticks, chunk_step, 0)
    for slot in range(2):
        ocopy(qt, 0, 0, slot).wait()
    put_small.wait()


def qkv_call(n, x2, wt, small, batch, seq, brow):
    tokens, d_model = x2.shape
    total = wt.shape[0]
    rows = 1024
    nchunks = total // rows
    cfg = (n, rows, batch, seq, nchunks, brow)
    o = jax.ShapeDtypeStruct((batch, total // 3, seq), jnp.bfloat16)
    return pl.pallas_call(
        functools.partial(qkv_kernel, cfg),
        out_shape=(o, o, o, jax.ShapeDtypeStruct((small.shape[0], d_model), jnp.bfloat16)),
        in_specs=[ANY] * 3,
        out_specs=(ANY,) * 4,
        scratch_shapes=[
            pltpu.VMEM((total, d_model), jnp.bfloat16),
            pltpu.VMEM((tokens, d_model), jnp.bfloat16),
            pltpu.VMEM((2, 256, d_model), jnp.bfloat16),
            pltpu.VMEM((small.shape[0], d_model), jnp.bfloat16),
            pltpu.VMEM((total, 128), jnp.float32),
            pltpu.VMEM((2, rows, seq), jnp.bfloat16),
            pltpu.SemaphoreType.DMA((2,)),
            pltpu.SemaphoreType.DMA((n,)),
            pltpu.SemaphoreType.DMA((n,)),
            pltpu.SemaphoreType.DMA((3,)),
            pltpu.SemaphoreType.DMA((2,)),
        ] + _sems(nchunks),
        compiler_params=pltpu.CompilerParams(collective_id=1, has_side_effects=True, vmem_limit_bytes=VMEM_LIMIT),
        name='qkv',
    )(x2, wt, small)


def attention_kernel(cfg, qt, kt, vt, *rest):
    n, head, gather_of, nref, nbuf, every = cfg
    wrefs, ctx, bufs = rest[:nref], rest[nref], rest[nref + 1:nref + 1 + nbuf]
    send, recv = rest[nref + 1 + nbuf:]
    step = pl.program_id(0) * pl.num_programs(1) + pl.program_id(1)
    w = Where(n)
    ga = gather_of(w, wrefs, bufs, send, recv)

    @pl.when(step == 0)
    def _():
        w.greet(False)
        ga.prelude()

    for t in range(ga.ticks):
        @pl.when(step == min((t + 1) * every, pl.num_programs(0) * pl.num_programs(1) - 1))
        def _():
            ga.tick(t)

    rows, seq = qt.shape[1], qt.shape[2]
    half = seq // 2
    c = (head ** -0.5) * LOG2E
    kpos = lax.broadcasted_iota(jnp.int32, (half, half), 0)
    qpos = lax.broadcasted_iota(jnp.int32, (half, half), 1)
    allowed = kpos <= qpos
    tn = (((0,), (0,)), ((), ()))
    for pair in range(rows // (2 * head)):
        outs = []
        for hh in range(2):
            r = pl.ds((2 * pair + hh) * head, head)
            q, k, v = qt[0, r, :], kt[0, r, :], vt[0, r, :]
            k_t = k.T
            s0 = jnp.dot(k_t[:half], q[:, :half], preferred_element_type=jnp.float32)
            s0 = jnp.where(allowed, s0, -jnp.inf)
            m0 = jnp.max(s0, axis=0, keepdims=True)
            e0 = jnp.exp2((s0 - m0) * c)
            p0 = (e0 * (1.0 / jnp.sum(e0, axis=0, keepdims=True))).astype(jnp.bfloat16)
            o0 = jnp.dot(v[:, :half], p0, preferred_element_type=jnp.float32)
            s1 = jnp.dot(k_t[:half], q[:, half:], preferred_element_type=jnp.float32)
            s2 = jnp.dot(k_t[half:], q[:, half:], preferred_element_type=jnp.float32)
            s2 = jnp.where(allowed, s2, -jnp.inf)
            m1 = jnp.maximum(jnp.max(s1, axis=0, keepdims=True), jnp.max(s2, axis=0, keepdims=True))
            e1 = jnp.exp2((s1 - m1) * c)
            e2 = jnp.exp2((s2 - m1) * c)
            inv = 1.0 / (jnp.sum(e1, axis=0, keepdims=True) + jnp.sum(e2, axis=0, keepdims=True))
            p1 = jnp.concatenate([(e1 * inv).astype(jnp.bfloat16), (e2 * inv).astype(jnp.bfloat16)], axis=0)
            o1 = jnp.dot(v, p1, preferred_element_type=jnp.float32)
            outs.append(jnp.concatenate([o0, o1], axis=1))
        o = jnp.concatenate(outs, axis=0)
        ctx[:, pl.ds(pair * 2 * head, 2 * head)] = o.T.astype(jnp.bfloat16)


def attention_call(n, qt, kt, vt, head, gather_of, wrefs, bufs, total, every):
    batch, d_model, seq = qt.shape
    rows = 256
    grid = (batch, d_model // rows)
    spec = pl.BlockSpec((1, rows, seq), lambda b, h: (b, h, 0))
    nref, nbuf = len(wrefs), len(bufs)
    out = pl.pallas_call(
        functools.partial(attention_kernel, (n, head, gather_of, nref, nbuf, every)),
        grid=grid,
        out_shape=(jax.ShapeDtypeStruct((batch * seq, d_model), jnp.bfloat16),) + tuple(bufs),
        in_specs=[spec] * 3 + [ANY] * nref,
        out_specs=(pl.BlockSpec((seq, rows), lambda b, h: (b, h)),) + (ANY,) * nbuf,
        scratch_shapes=_sems(total),
        compiler_params=pltpu.CompilerParams(collective_id=2, has_side_effects=True, vmem_limit_bytes=VMEM_LIMIT),
        name='attention',
    )(qt, kt, vt, *wrefs)
    return out[0], list(out[1:])


def load_parts(n, f, buf, own, dst, sem, start):
    depth = own.shape[0]
    if not start:
        pltpu.make_async_copy(buf, dst, sem).wait()
        return
    for r in range(n):
        dev = lax.rem(f + r, n)
        rows = pl.ds(pl.multiple_of(dev * depth, depth), depth)
        pltpu.make_async_copy(own if r == 0 else buf.at[rows, :], dst.at[rows, :], sem).start()


def out_kernel(cfg, ctx, x, small, wo_own, *rest):
    n, nwo, gather_of, nref, nbuf, every, rows_of = cfg
    wo, rest = rest[:nwo], rest[nwo:]
    wrefs, (x1, h2), bufs = rest[:nref], rest[nref:nref + 2], rest[nref + 2:nref + 2 + nbuf]
    wv, lsem, send, recv = rest[nref + 2 + nbuf:]
    i = pl.program_id(0)
    w = Where(n)
    ga = gather_of(w, wrefs, bufs, send, recv)
    width = wv.shape[1] // nwo

    @pl.when(i == 0)
    def _():
        w.greet(False)
        ga.prelude()
        for start in (True, False):
            for c in range(nwo):
                cols = pl.ds(c * width, width)
                load_parts(n, w.f, wo[c], wo_own.at[:, cols], wv.at[:, cols], lsem.at[c], start)

    for t in range(ga.ticks):
        @pl.when(i == min((t + 1) * every, pl.num_programs(0) - 1))
        def _():
            ga.tick(t)

    bo, g2, b2 = (small[pl.ds(r, 1), :].astype(jnp.float32) for r in rows_of)
    acc = jnp.dot(ctx[...], wv[...], preferred_element_type=jnp.float32)
    y = (x[...].astype(jnp.float32) + acc + bo).astype(jnp.bfloat16)
    x1[...] = y
    h2[...] = _ln(y.astype(jnp.float32), g2, b2)


def out_call(n, ctx, x2, small, wo_own, wo, gather_of, wrefs, bufs, total, every, rows_of):
    tokens, d_model = x2.shape
    m = 256
    blk = pl.BlockSpec((m, d_model), lambda i: (i, 0))
    o = jax.ShapeDtypeStruct((tokens, d_model), jnp.bfloat16)
    nref, nbuf = len(wrefs), len(bufs)
    out = pl.pallas_call(
        functools.partial(out_kernel, (n, len(wo), gather_of, nref, nbuf, every, rows_of)),
        grid=(tokens // m,),
        out_shape=(o, o) + tuple(bufs),
        in_specs=[blk, blk, pl.BlockSpec(small.shape, lambda i: (0, 0)), ANY] + [ANY] * (len(wo) + nref),
        out_specs=(blk, blk) + (ANY,) * nbuf,
        scratch_shapes=[pltpu.VMEM((ctx.shape[1], d_model), jnp.bfloat16), pltpu.SemaphoreType.DMA((len(wo),))] + _sems(total),
        compiler_params=pltpu.CompilerParams(collective_id=3, has_side_effects=True, vmem_limit_bytes=VMEM_LIMIT),
        name='outproj',
    )(ctx, x2, small, wo_own, *wo, *wrefs)
    return out[0], out[1], list(out[2:])


def mm_kernel(cfg, a, bias, res, own, *rest):
    n, epilogue, npre, nnew, gather_of, nref, nbuf, tick_at, ready_at = cfg
    pre, rest = rest[:npre], rest[npre:]
    wrefs, rest = rest[:nref], rest[nref:]
    out, bufs = rest[0], rest[1:1 + nbuf]
    wv, lsem, send, recv = rest[1 + nbuf:]
    chunks = list(pre) + list(bufs[:nnew])
    j, i = pl.program_id(0), pl.program_id(1)
    ni = pl.num_programs(1)
    step = j * ni + i
    w = Where(n)
    ga = gather_of(w, wrefs, bufs, send, recv) if gather_of is not None else None
    width = wv.shape[2]

    def load(c, start):
        load_parts(n, w.f, chunks[c], own.at[:, pl.ds(c * width, width)], wv.at[c % 2], lsem.at[c % 2], start)

    @pl.when(step == 0)
    def _():
        load(0, True)
        if ga is not None:
            w.greet(False)
            ga.prelude()

    if ga is not None:
        for t in range(ga.ticks):
            @pl.when(step == tick_at[t])
            def _():
                ga.tick(t)

    for c in range(len(chunks)):
        @pl.when(jnp.logical_and(j == c, i == 0))
        def _():
            load(c, False)

        if c + 1 < len(chunks):
            @pl.when(jnp.logical_and(j == c, i == ni - 1))
            def _():
                load(c + 1, True)

    acc = jnp.dot(a[...], wv[lax.rem(j, 2)], preferred_element_type=jnp.float32)
    acc = acc + bias[...].astype(jnp.float32)
    if epilogue == 'gelu':
        out[...] = jax.nn.gelu(acc, approximate=True).astype(jnp.bfloat16)
    else:
        out[...] = (res[...].astype(jnp.float32) + acc).astype(jnp.bfloat16)


def mm_call(n, name, cid, a, bias, res, own, pre, new, m, width, epilogue, gather_of, wrefs, bufs, total, tick_at):
    tokens, k = a.shape
    nout = own.shape[1]
    nj, ni = nout // width, tokens // m
    comm = gather_of is not None
    nref, nbuf = len(wrefs), len(bufs)
    res_spec = pl.BlockSpec((m, width), lambda j, i: (i, j)) if epilogue != 'gelu' else pl.BlockSpec((16, 128), lambda j, i: (0, 0))
    out = pl.pallas_call(
        functools.partial(mm_kernel, (n, epilogue, len(pre), new, gather_of, nref, nbuf, tick_at, None)),
        grid=(nj, ni),
        out_shape=(jax.ShapeDtypeStruct((tokens, nout), jnp.bfloat16),) + tuple(bufs),
        in_specs=[pl.BlockSpec((m, k), lambda j, i: (i, 0)), pl.BlockSpec((1, width), lambda j, i: (0, j)), res_spec, ANY] + [ANY] * (len(pre) + nref),
        out_specs=(pl.BlockSpec((m, width), lambda j, i: (i, j)),) + (ANY,) * nbuf,
        scratch_shapes=[pltpu.VMEM((2, k, width), jnp.bfloat16), pltpu.SemaphoreType.DMA((2,))] + _sems(max(total, 1)),
        compiler_params=pltpu.CompilerParams(collective_id=cid, has_side_effects=True, vmem_limit_bytes=VMEM_LIMIT) if comm else pltpu.CompilerParams(vmem_limit_bytes=VMEM_LIMIT),
        name=name,
    )(a, bias, res, own, *pre, *wrefs)
    return out[0], list(out[1:])


def solution(mesh):
    batch_axes = ('dp', 'fsdp')
    n = mesh.shape['fsdp']

    def local_layer(prompts, ln1_gain, ln1_bias, w_qkv, b_qkv, w_out, b_out, ln2_gain, ln2_bias, w_up, b_up, w_down, b_down):
        batch, seq, d_model = prompts.shape
        heads, head = w_qkv.shape[2], w_qkv.shape[3]
        ffn = w_up.shape[1]
        depth = d_model // n
        x2 = prompts.reshape(batch * seq, d_model)
        wt = w_qkv.transpose(1, 2, 3, 0).reshape(3 * heads * head, depth)

        vecs = [ln1_gain, ln1_bias, b_out, ln2_gain, ln2_bias, b_down, b_qkv, b_up]
        small = jnp.concatenate([v.reshape(-1, depth) for v in vecs], axis=0)
        brow = 6
        urow = brow + b_qkv.shape[0] // depth
        nrow = urow + b_up.shape[0] // depth
        small = jnp.pad(small, ((0, -nrow % 16), (0, 0)))

        qt, kt, vt, small = qkv_call(n, x2, wt, small, batch, seq, brow)

        cu = 1024
        cd = d_model // 4
        up_buf = jax.ShapeDtypeStruct((d_model, cu), jnp.bfloat16)
        dn_buf = jax.ShapeDtypeStruct((ffn, cd), jnp.bfloat16)

        def up_gather(first, count):
            def make(w, wrefs, bufs, send, recv):
                return Gather(w, count, _row_src([(wrefs[0], (first + c) * cu, cu) for c in range(count)]), _row_dst(bufs, depth), send, recv)
            return make

        n2, n3 = 3, 2
        nwo = d_model // cu

        def attn_gather(w, wrefs, bufs, send, recv):
            parts = [(wrefs[0], c * cu, cu) for c in range(nwo)] + [(wrefs[1], c * cu, cu) for c in range(n2)]
            return Gather(w, nwo + n2, _row_src(parts), _row_dst(bufs, depth), send, recv)

        ctx, got = attention_call(n, qt, kt, vt, head, attn_gather, [w_out, w_up], [up_buf] * (nwo + n2), nwo + n2, 3)
        wo, up = got[:nwo], got[nwo:]
        x1, h2, got = out_call(n, ctx, x2, small, w_out, wo, up_gather(n2, n3), [w_up], [up_buf] * n3, n3, 1, (2, 3, 4))
        up += got

        nup = ffn // cu
        left = nup - n2 - n3
        ndn = d_model // cd
        nd4 = 2

        def dn_parts(wref, first, count, bufs):
            u = wref.shape[0] // 4
            kd = wref.shape[0]

            def src(c, q, m):
                return wref.at[pl.ds(pl.multiple_of(q * u, u), m * u), pl.ds((first + c) * cd, cd)]

            def dst(c, dev, q, m):
                return bufs[c].at[pl.ds(pl.multiple_of(dev * kd + q * u, u), m * u), :]

            return src, dst

        def mlp_gather(w, wrefs, bufs, send, recv):
            usrc = _row_src([(wrefs[0], (n2 + n3 + c) * cu, cu) for c in range(left)])
            udst = _row_dst(bufs[:left], depth)
            dsrc, ddst = dn_parts(wrefs[1], 0, nd4, bufs[left:])
            return Gather(
                w, left + nd4,
                lambda c, q, m: usrc(c, q, m) if c < left else dsrc(c - left, q, m),
                lambda c, dev, q, m: udst(c, dev, q, m) if c < left else ddst(c - left, dev, q, m),
                send, recv)

        def down_gather(w, wrefs, bufs, send, recv):
            src, dst = dn_parts(wrefs[0], nd4, ndn - nd4, bufs)
            return Gather(w, ndn - nd4, src, dst, send, recv)

        b_up_row = small[urow:urow + ffn // d_model].reshape(ffn // d_model, n, depth).transpose(1, 0, 2).reshape(1, ffn)
        b_dn_row = small[5:6]
        hid, got = mm_call(
            n, 'mlpup', 4, h2, b_up_row, h2, w_up, up, left, 512, cu, 'gelu', mlp_gather, [w_up, w_down],
            [up_buf] * left + [dn_buf] * nd4, left + nd4, [4, 8, 12, 16, 19, 23, 27, 31])
        dn = got[left:]
        y, _ = mm_call(
            n, 'mlpdown', 5, hid, b_dn_row, x1, w_down, dn, ndn - nd4, 512, cd, 'residual', down_gather, [w_down],
            [dn_buf] * (ndn - nd4), ndn - nd4, [2, 4, 6, 7, 11])

        def cache(t):
            return t.reshape(batch, heads, head, seq).transpose(0, 3, 1, 2)

        return y.reshape(batch, seq, d_model), cache(kt), cache(vt)

    weight_spec = P('fsdp')
    return jax.shard_map(local_layer, mesh=mesh, in_specs=(P(batch_axes),) + (weight_spec,) * 12, out_specs=(P(batch_axes), P(batch_axes), P(batch_axes)), check_vma=False)
```

time: 593 us -> 561 us (0.946)
  Pallas kernels: 0 us -> 526 us
  matrix products: 386 us -> 0 us
  blocking collectives: 82.4 us -> 0 us
  waiting for transfers between devices: 51.1 us -> 0 us
  other arithmetic: 20.5 us -> 0 us
  between operations: 14.2 us -> 0.68 us
    pallas_call x0 -> x5, Pallas kernels: none -> 526 us  [the longest x2 257 us: mm_call(): pl.pallas_call(functools.partial(mm_kernel, (n, epilogue, len(pre), new,...]
    dot_general x6 -> x0, matrix products: 319 us -> none  [the longest x1 98.2 us: local_layer(): jnp.einsum('bsd,df->bsf', normed2, w_up_full, preferred_element_type=jnp....]
    all_gather x8 -> x0, blocking collectives: 82.4 us -> none  [gather_full(): return lax.all_gather(shard, 'fsdp', axis=0, tiled=True)]
    sub x2 -> x0, matrix products: 67.8 us -> none  [one_block(): probs = jax.nn.softmax(scores, axis=-1).astype(jnp.bfloat16)]
    all_gather x4 -> x0, waiting for transfers between devices: 48.3 us -> none  [gather_full(): return lax.all_gather(shard, 'fsdp', axis=0, tiled=True)]
    unnamed x37 -> x3, local copies, waits for them, and re-layouts: 4.05 us -> 24.2 us
    reduce_sum x4 -> x0, other arithmetic: 17.1 us -> none  [the longest x2 9.08 us: layer_norm(): mean_val = jnp.mean(act_f32, axis=-1, keepdims=True)]
    squeeze x1 -> x0, local copies, waits for them, and re-layouts: 16.7 us -> none  [local_layer(): ctx_blocks = causal_attention(proj_qkv[0], proj_qkv[1], proj_qkv[2])]
  transfers between devices with their start and end apart: 4 -> 0, of which waited for: 2 -> 0; matrix products, arithmetic and copies ran while one was open for 60% -> 0% of each run, Pallas kernels for 0% -> 0%
where the time goes in v1:
time: 561 us; the launch traced here: 560 us
  Pallas kernels  526 us (94%)
  local copies, waits for them, and re-layouts  33.1 us (6%)
    pallas_call x2, Pallas kernels, mm_call(): pl.pallas_call(functools.partial(mm_kernel, (n, epilogue, len(pre), new,...  257 us
    pallas_call x1, Pallas kernels, qkv_call(): pl.pallas_call(functools.partial(qkv_kernel, cfg), out_shape=(o, o, o, ja...  113 us
    pallas_call x1, Pallas kernels, attention_call(): pl.pallas_call(functools.partial(attention_kernel, (n, head, gather_of, n...  103 us
    pallas_call x1, Pallas kernels, out_call(): pl.pallas_call(functools.partial(out_kernel, (n, len(wo), gather_of, nref...  53.9 us
    unnamed x3, local copies, waits for them, and re-layouts  24.2 us

profile of v1, /device:TPU:81, one launch (start us, length us, event | category | flops | bytes accessed | tf_op | source)
XLA Modules:
  0.0 559.8 jit_solution(7519704189888834165)
XLA Ops:
  0.6 0.7 reshape.53
  1.3 0.7 reshape.54
  1.9 0.7 reshape.55
  2.6 0.7 reshape.56
  3.3 0.7 reshape.57
  3.9 0.7 reshape.58
  4.6 0.7 reshape.59
  5.3 0.7 reshape.60
  6.0 0.1 concatenate.3
  6.1 0.6 pad.4.small_ref
  6.7 112.8 %qkv.1 = (bf16[4,2048,512]{2,1,0:T(8,128)(2,1)}, bf16[4,2048,512]{2,1,0:T(8,128)(2,1)}, bf16[4,2048,512]{2,1,0:T(8,128)(2,1)}, bf16[16,2048]{1,0:T(8,128)(2,1)}) custom-call(bf16[2048,2048]{1,0:T(8,128)(2,1)} %bitcast.14, bf16[6144,256]{1,0:T(8,128)(2,1)} %bitcast.19, bf16[16,256]{1,0:T(8,128)(2,1)} %pad.4.small_ref), custom_call_target="tpu_custom_call" | custom-call | tf_op jit(solution)/shard_map/qkv/pallas_call | solution.py:272
  119.5 1.4 slice.7.bias
  120.9 0.8 slice.6
  121.7 0.6 reshape.62.bias
  122.3 102.6 %attention.1 = (bf16[2048,2048]{1,0:T(8,128)(2,1)}, bf16[2048,1024]{1,0:T(8,128)(2,1)}, bf16[2048,1024]{1,0:T(8,128)(2,1)}, bf16[2048,1024]{1,0:T(8,128)(2,1)}, ...) custom-call(bf16[4,2048,512]{2,1,0:T(8,128)(2,1)} %get-tuple-element.21.qt, ...), custom_call_target="tpu_custom_call" | custom-call | tf_op jit(solution)/shard_map/attention/pallas_call | solution.py:352
  224.9 53.9 %outproj.1 = (bf16[2048,2048]{1,0:T(8,128)(2,1)}, bf16[2048,2048]{1,0:T(8,128)(2,1)}, bf16[2048,1024]{1,0:T(8,128)(2,1)}, bf16[2048,1024]{1,0:T(8,128)(2,1)}) custom-call(bf16[2048,2048]{1,0:T(8,128)(2,1)} %get-tuple-element.24.ctx, bf16[2048,2048]{1,0:T(8,128)(2,1)} %bitcast.15, bf16[16,2048]{1,0:T(8,128)(2,1)} %get-tuple-element.25.small, ...), custom_call_target="tpu_custom_call" | custom-call | tf_op jit(solution)/shard_map/outproj/pallas_call | solution.py:413
  278.8 129.5 %mlpup.1 = (bf16[2048,8192]{1,0:T(8,128)(2,1)}, bf16[2048,1024]{1,0:T(8,128)(2,1)}, bf16[2048,1024]{1,0:T(8,128)(2,1)}, bf16[2048,1024]{1,0:T(8,128)(2,1)}, bf16...) custom-call(bf16[2048,2048]{1,0:T(8,128)(2,1)} %get-tuple-element.28.a.res, bf16[1,8192]{1,0:T(2,128)(2,1)} %reshape.62.bias, ...), custom_call_target="tpu_custom_call" | custom-call | tf_op jit(solution)/shard_map/mlpup/pallas_call | solution.py:481
  408.3 127.2 %mlpdown.1 = (bf16[2048,2048]{1,0:T(8,128)(2,1)}, bf16[8192,512]{1,0:T(8,128)(2,1)}, bf16[8192,512]{1,0:T(8,128)(2,1)}) custom-call(bf16[2048,8192]{1,0:T(8,128)(2,1)} %get-tuple-element.34.a, bf16[1,2048]{1,0:T(2,128)(2,1)} %slice.7.bias, bf16[2048,2048]{1,0:T(8,128)(2,1)} %get-tuple-element.35.res, bf16[1024,2048]{1,0:T(8,128)(2,1)} %rest_2_.3, ...), custom_call_target="tpu_custom_call" | custom-call | tf_op jit(solution)/shard_map/mlpdown/pallas_call | solution.py:481
  535.6 8.4 %copy.20 = bf16[4,512,2048]{2,1,0:T(8,128)(2,1)} copy(bf16[4,512,2048]{2,1,0:T(8,128)(2,1)} %bitcast.18) | data formatting | bytes 16777216
  544.0 7.9 %copy.21 = bf16[4,512,32,64]{1,3,2,0:T(8,128)(2,1)} copy(bf16[4,512,32,64]{1,3,2,0:T(8,128)(2,1)} %bitcast.17) | data formatting | bytes 16777216
  551.9 7.9 %copy.22 = bf16[4,512,32,64]{1,3,2,0:T(8,128)(2,1)} copy(bf16[4,512,32,64]{1,3,2,0:T(8,128)(2,1)} %bitcast.16) | data formatting | bytes 16777216
